TPU v7x, 32 devices: a whole 2x2x4 slice. The times are simulated.
32 devices in a mesh: ma: 16 (over z, x, core), af: 2 (over y).
Axes of the slice: x: 2, y: 2, z: 4, core: 2. Of those that a mesh axis runs over, the one named last changes fastest.
Arguments:
- coeffs: bfloat16 [512, 128, 2049], P('ma', 'af'), parts along dimension 1, may hold values from -6 to 6
- legendre: bfloat16 [512, 256, 2049], P('ma'), may hold values from -0.1875 to 0.1875
- assign: int32 [512], P('ma'), may hold values from 0 to 511, each once
Outputs:
- fourier: float32 [512, 128, 1024], P('ma', 'af'), parts along dimension 1
There are 2 independent parts, one for each index of `af`. A program takes and returns all parts, laid end to end along the dimension named above; an argument that names none is the same for every part. Nothing has to cross between parts.
Inputs may be any that keep to these rules, and one draw needn't show every extreme that they name: Slot s carries the wavenumbers assign[s] and 2047 - assign[s]; every pair appears once.
All inputs are finite; a program needn't handle non-finite values.
Results may differ from a plain program's by a relative error of at most 0.0003.
Values sent between devices are 32-bit elements; how exact they have to be, the bound alone decides.
A program may use at most 128 MiB of HBM per device.

v0:
```python
import functools

import jax
import jax.numpy as jnp
from jax import lax
from jax.experimental import pallas as pl
from jax.experimental.pallas import tpu as pltpu
from jax.sharding import PartitionSpec as P

TRUNC = 2047
ROWS_PER_STEP = 4
PIECES = 4
FIRST_PIECES = 1
LAST_PIECES = 1


def group_kernel(pairs_ref, coeff_ref, out_ref, *, start):
    held, columns, width = coeff_ref.shape
    pack = 16
    for slot in range(held):
        pair = pairs_ref[start + pl.program_id(0) * held + slot]
        group_slot(TRUNC + 1 - pair, coeff_ref.at[slot], out_ref.at[slot], pack)


def group_slot(first_len, coeff_ref, out_ref, pack):
    columns, width = coeff_ref.shape
    entry = lax.broadcasted_iota(jnp.int32, (pack, width), 1)
    first = entry < first_len
    odd_gap = (jnp.where(first, entry, entry - first_len) & 1) == 1
    sign = jnp.where(odd_gap, -1.0, 1.0)
    scales = [
        jnp.where(first, 1.0, 0.0),
        jnp.where(first, 0.0, 1.0),
        jnp.where(first, sign, 0.0),
        jnp.where(first, 0.0, sign),
    ]
    scales = [scale.astype(out_ref.dtype) for scale in scales]
    for low in range(0, columns, pack):
        values = coeff_ref[low:low + pack, :]
        for index, scale in enumerate(scales):
            at = index * columns + low
            out_ref[at:at + pack, :] = values * scale


def group_rows(coeffs, assign, start, part):
    _, columns, width = coeffs.shape
    held = 2 if part % 2 == 0 and start % 2 == 0 else 1
    return pl.pallas_call(
        functools.partial(group_kernel, start=start),
        grid_spec=pltpu.PrefetchScalarGridSpec(
            num_scalar_prefetch=1,
            grid=(part // held,),
            in_specs=[pl.BlockSpec((held, columns, width), lambda i, p: (start // held + i, 0, 0))],
            out_specs=pl.BlockSpec((held, 4 * columns, width), lambda i, p: (i, 0, 0)),
        ),
        out_shape=jax.ShapeDtypeStruct((part, 4 * columns, width), coeffs.dtype),
        cost_estimate=pl.CostEstimate(flops=0, transcendentals=0, bytes_accessed=part * columns * width * 10),
        name="group_rows",
    )(assign, coeffs)


def band_kernel(own_ref, *refs, band):
    out_ref = refs[-1]
    bands = out_ref.shape[0]
    south = pl.program_id(0)
    at = 0
    for value_ref in refs[:-1]:
        for slot in range(value_ref.shape[0]):
            rows = value_ref[slot].T
            for index in range(bands):
                to = jnp.where(south == 1, bands - 1 - index, index)
                out_ref[to, :band, at, :] = rows[index * band:(index + 1) * band]
            at += 1
    if out_ref.shape[1] > band:
        own = jnp.broadcast_to(own_ref[...], (bands, 1, at, own_ref.shape[-1]))
        out_ref[:, band:] = own


def band_rows(values, own, devices, extra):
    _, lanes, lat_half = values[0].shape
    part = sum(value.shape[0] for value in values)
    lanes //= 2
    bands = devices // 2
    band = lat_half // bands
    return pl.pallas_call(
        functools.partial(band_kernel, band=band),
        grid=(2,),
        in_specs=[pl.BlockSpec((1, lanes), lambda i: (0, 0))]
        + [pl.BlockSpec((value.shape[0], lanes, lat_half), lambda i: (0, i, 0)) for value in values],
        out_specs=pl.BlockSpec((bands, band + extra, part, lanes), lambda i: (i, 0, 0, 0)),
        out_shape=jax.ShapeDtypeStruct((devices, band + extra, part, lanes), jnp.float32),
        cost_estimate=pl.CostEstimate(
            flops=0, transcendentals=0, bytes_accessed=part * lanes * lat_half * 16
        ),
        name="band_rows",
    )(own, *values)


def chunk_rows(coeffs, legendre, assign, own, pieces, devices, extra):
    values = []
    for start, part in pieces:
        groups = group_rows(coeffs, assign, start, part)
        functions = lax.optimization_barrier(legendre[start:start + part])
        value = jnp.einsum("sgk,shk->sgh", groups, functions, preferred_element_type=jnp.float32)
        value, coeffs, legendre = lax.optimization_barrier((value, coeffs, legendre))
        values.append(value)
    return band_rows(values, own, devices, extra)


def place_kernel(flip_ref, pairs_ref, *refs, held):
    out_ref, place = refs[-2:]
    value_refs = refs[:-3] if held else refs[:-2]
    devices, rows, _, lanes = value_refs[0].shape
    count, total = place.shape
    total //= 2
    columns = lanes // 2

    @pl.when(pl.program_id(0) == 0)
    def _():
        pairs = jnp.broadcast_to(pairs_ref[...], (count, total))
        lane = lax.broadcasted_iota(jnp.int32, (count, total), 1)
        place[:, :total] = (pairs == lane).astype(jnp.bfloat16)
        place[:, total:] = (total - 1 - pairs == lane).astype(jnp.bfloat16)

    def by_lane(row):
        tiles = [ref[:, row].reshape(devices * ref.shape[2], lanes).T for ref in value_refs]
        return tiles[0] if len(tiles) == 1 else jnp.concatenate(tiles, axis=1)

    flip = flip_ref[0]
    values = jnp.concatenate([by_lane(row)[None] for row in range(rows)], axis=0)
    for half in range(2):
        mine = values[:, half * columns:(half + 1) * columns].reshape(rows * columns, count)
        high = mine.astype(jnp.bfloat16)
        low = (mine - high.astype(jnp.float32)).astype(jnp.bfloat16)
        span = slice(half * total, (half + 1) * total)
        placed = jnp.dot(high, place[:, span], preferred_element_type=jnp.float32)
        placed += jnp.dot(low, place[:, span], preferred_element_type=jnp.float32)
        placed = placed.reshape(rows, columns, total)
        for row in range(rows):
            to = jnp.where(flip == 1, rows - 1 - row, row)
            block = placed[row]
            if held:
                block += refs[-3][to, :, span]
            out_ref[to, :, span] = block


def place_columns(received, pairs, flip, band, total, placed):
    devices, _, _, lanes = received[0].shape
    count = pairs.shape[0]
    held = placed is not None
    steps = band // ROWS_PER_STEP
    columns = lanes // 2
    out_spec = pl.BlockSpec(
        (ROWS_PER_STEP, columns, 2 * total),
        lambda i, f: (jnp.where(f[0] == 1, steps - 1 - i, i), 0, 0),
    )
    return pl.pallas_call(
        functools.partial(place_kernel, held=held),
        grid_spec=pltpu.PrefetchScalarGridSpec(
            num_scalar_prefetch=1,
            grid=(steps,),
            in_specs=[pl.BlockSpec((count, 1), lambda i, f: (0, 0))]
            + [
                pl.BlockSpec((devices, ROWS_PER_STEP, block.shape[2], lanes), lambda i, f: (0, i, 0, 0))
                for block in received
            ]
            + ([out_spec] if held else []),
            out_specs=out_spec,
            scratch_shapes=[pltpu.VMEM((count, 2 * total), jnp.bfloat16)],
        ),
        out_shape=jax.ShapeDtypeStruct((band, columns, 2 * total), jnp.float32),
        cost_estimate=pl.CostEstimate(
            flops=4 * band * columns * count * total, transcendentals=0, bytes_accessed=32 * band * columns * total
        ),
        name="place_columns",
    )(flip, pairs, *received, *([placed] if held else []))


def shards(coeffs, legendre, assign):
    devices = lax.axis_size("ma")
    slots, columns, _ = coeffs.shape
    band = 2 * legendre.shape[1] // devices
    piece = max(slots // PIECES, 1)
    starts = list(range(0, slots, piece))
    bounds = [0, FIRST_PIECES, len(starts) - LAST_PIECES, len(starts)]
    own = jnp.pad(assign.astype(jnp.float32), (0, 2 * columns - slots))[None, :]
    flip = (lax.axis_index("ma") >= devices // 2).astype(jnp.int32)[None]
    received = []
    parts = []
    for low, high in zip(bounds, bounds[1:]):
        extra = 1 if low == 0 else 0
        pieces = [(start, min(piece, slots - start)) for start in starts[low:high]]
        rows = chunk_rows(coeffs, legendre, assign, own, pieces, devices, extra)
        rows, coeffs, legendre = lax.optimization_barrier((rows, coeffs, legendre))
        received.append(lax.all_to_all(rows, "ma", 0, 0, tiled=True))
        parts.append(sum(part for _, part in pieces))
    all_pairs = received[0][:, band, 0, :slots].astype(jnp.int32)
    ends = [sum(parts[:n]) for n in range(len(parts) + 1)]
    pairs = [all_pairs[:, low:high].reshape(-1, 1) for low, high in zip(ends, ends[1:])]
    early = jnp.concatenate(pairs[:-1], axis=0)
    placed = place_columns(received[:-1], early, flip, band, devices * slots, None)
    return place_columns(received[-1:], pairs[-1], flip, band, devices * slots, placed)


def solution(mesh):
    return jax.shard_map(
        shards,
        mesh=mesh,
        in_specs=(P("ma", "af", None), P("ma", None, None), P("ma")),
        out_specs=P("ma", "af", None),
        check_vma=False,
    )
```

profile of v0, /device:TPU:15, one launch (start us, length us, event | category | flops | bytes accessed | tf_op | source)
XLA Modules:
  0.0 238.6 jit_solution(9625184792470976488)
XLA Ops:
  0.0 0.7 convert_element_type.12
  0.7 0.5 pad_bitcast_fusion.own_ref
  1.1 6.5 %group_rows.4 = bf16[8,256,2049]{2,1,0:T(8,128)(2,1)} custom-call(s32[32]{0:T(128)} %pairs_ref.7, bf16[32,64,2049]{2,1,0:T(8,128)(2,1)} %coeff_ref.4), custom_call_target="tpu_custom_call" | custom-call | bytes 10490880 | tf_op jit(solution)/shard_map/group_rows/pallas_call | solution.py:48
  7.6 0.0 slice-start
  7.6 3.4 %slice-done = bf16[8,256,2049]{1,0,2:T(8,128)(2,1)S(1)} async-done(((bf16[32,256,2049]{1,0,2:T(8,128)(2,1)}), bf16[8,256,2049]{1,0,2:T(8,128)(2,1)S(1)}, s32[]{:S(2)}) %slice-start) | async-done | bytes 8392728 | tf_op jit(solution)/shard_map/slice | solution.py:103
  11.0 7.5 %fusion.6.refs_0_ = f32[8,256,256]{2,1,0:T(8,128)} fusion(bf16[8,256,2049]{2,1,0:T(8,128)(2,1)} %group_rows.4, bf16[8,256,2049]{1,0,2:T(8,128)(2,1)S(1)} %slice-done), kind=kOutput, calls=%fused_computation.6 | convolution fusion | flops 2148532224 | bytes 18882560 | tf_op jit(solution)/shard_map/sgk,shk->sgh/dot_general | solution.py:104
  18.5 4.2 %band_rows.3 = f32[16,33,8,128]{3,2,1,0:T(8,128)} custom-call(f32[1,128]{1,0:T(1,128)} %pad_bitcast_fusion.own_ref, f32[8,256,256]{2,1,0:T(8,128)} %fusion.6.refs_0_), custom_call_target="tpu_custom_call" | custom-call | bytes 4194304 | tf_op jit(solution)/shard_map/band_rows/pallas_call | solution.py:85
  22.6 6.5 %all-to-all-start = ((f32[16,33,8,128]{3,2,1,0:T(8,128)}), f32[16,33,8,128]{3,2,1,0:T(8,128)S(1)}, u32[]{:S(2)}, u32[]{:S(2)}) async-start(f32[16,33,8,128]{3,2,1,0:T(8,128)} %band_rows.3), calls=%async_computation | async-start | bytes 4325376 | tf_op jit(solution)/shard_map/all_to_all | solution.py:195
  29.2 6.5 %group_rows.5 = bf16[8,256,2049]{2,1,0:T(8,128)(2,1)} custom-call(s32[32]{0:T(128)} %pairs_ref.7, bf16[32,64,2049]{2,1,0:T(8,128)(2,1)} %coeff_ref.4), custom_call_target="tpu_custom_call" | custom-call | bytes 10490880 | tf_op jit(solution)/shard_map/group_rows/pallas_call | solution.py:48
  35.6 0.0 slice-start.1
  35.6 3.4 %slice-done.1 = bf16[8,256,2049]{1,0,2:T(8,128)(2,1)S(1)} async-done(((bf16[32,256,2049]{1,0,2:T(8,128)(2,1)}), bf16[8,256,2049]{1,0,2:T(8,128)(2,1)S(1)}, s32[]{:S(2)}) %slice-start.1) | async-done | bytes 8392728 | tf_op jit(solution)/shard_map/slice | solution.py:103
  39.0 7.6 %fusion.4.refs_0_ = f32[8,256,256]{2,1,0:T(8,128)} fusion(bf16[8,256,2049]{2,1,0:T(8,128)(2,1)} %group_rows.5, bf16[8,256,2049]{1,0,2:T(8,128)(2,1)S(1)} %slice-done.1), kind=kOutput, calls=%fused_computation.4 | convolution fusion | flops 2148532224 | bytes 18882560 | tf_op jit(solution)/shard_map/sgk,shk->sgh/dot_general | solution.py:104
  46.6 6.5 %group_rows.6 = bf16[8,256,2049]{2,1,0:T(8,128)(2,1)} custom-call(s32[32]{0:T(128)} %pairs_ref.7, bf16[32,64,2049]{2,1,0:T(8,128)(2,1)} %coeff_ref.4), custom_call_target="tpu_custom_call" | custom-call | bytes 10490880 | tf_op jit(solution)/shard_map/group_rows/pallas_call | solution.py:48
  53.0 0.0 slice-start.2
  53.0 3.4 %slice-done.2 = bf16[8,256,2049]{1,0,2:T(8,128)(2,1)S(1)} async-done(((bf16[32,256,2049]{1,0,2:T(8,128)(2,1)}), bf16[8,256,2049]{1,0,2:T(8,128)(2,1)S(1)}, s32[]{:S(2)}) %slice-start.2) | async-done | bytes 8392728 | tf_op jit(solution)/shard_map/slice | solution.py:103
  56.4 7.5 %fusion.2.refs_1_ = f32[8,256,256]{2,1,0:T(8,128)} fusion(bf16[8,256,2049]{2,1,0:T(8,128)(2,1)} %group_rows.6, bf16[8,256,2049]{1,0,2:T(8,128)(2,1)S(1)} %slice-done.2), kind=kOutput, calls=%fused_computation.2 | convolution fusion | flops 2148532224 | bytes 18882560 | tf_op jit(solution)/shard_map/sgk,shk->sgh/dot_general | solution.py:104
  63.9 6.7 %band_rows.4 = f32[16,32,16,128]{3,2,1,0:T(8,128)} custom-call(f32[1,128]{1,0:T(1,128)} %pad_bitcast_fusion.own_ref, f32[8,256,256]{2,1,0:T(8,128)} %fusion.4.refs_0_, f32[8,256,256]{2,1,0:T(8,128)} %fusion.2.refs_1_), custom_call_target="tpu_custom_call" | custom-call | bytes 8388608 | tf_op jit(solution)/shard_map/band_rows/pallas_call | solution.py:85
  70.6 7.4 %all-to-all-done.refs_0_ = f32[16,33,8,128]{3,2,1,0:T(8,128)S(1)} async-done(((f32[16,33,8,128]{3,2,1,0:T(8,128)}), f32[16,33,8,128]{3,2,1,0:T(8,128)S(1)}, u32[]{:S(2)}, u32[]{:S(2)}) %all-to-all-start) | async-done | bytes 2162720 | tf_op jit(solution)/shard_map/all_to_all | solution.py:195
  78.0 0.0 copy-start
  78.0 4.8 %all-to-all-start.2 = ((f32[16,32,16,128]{3,2,1,0:T(8,128)}), f32[16,32,16,128]{3,2,1,0:T(8,128)}, u32[]{:S(2)}, u32[]{:S(2)}) async-start(f32[16,32,16,128]{3,2,1,0:T(8,128)} %band_rows.4), calls=%async_computation.2 | async-start | bytes 8388608 | tf_op jit(solution)/shard_map/all_to_all | solution.py:195
  82.8 6.5 %group_rows.7 = bf16[8,256,2049]{2,1,0:T(8,128)(2,1)} custom-call(s32[32]{0:T(128)} %pairs_ref.7, bf16[32,64,2049]{2,1,0:T(8,128)(2,1)} %coeff_ref.4), custom_call_target="tpu_custom_call" | custom-call | bytes 10490880 | tf_op jit(solution)/shard_map/group_rows/pallas_call | solution.py:48
  89.2 0.0 slice-start.3
  89.2 3.4 %slice-done.3 = bf16[8,256,2049]{1,0,2:T(8,128)(2,1)S(1)} async-done(((bf16[32,256,2049]{1,0,2:T(8,128)(2,1)}), bf16[8,256,2049]{1,0,2:T(8,128)(2,1)S(1)}, s32[]{:S(2)}) %slice-start.3) | async-done | bytes 8392728 | tf_op jit(solution)/shard_map/slice | solution.py:103
  92.6 7.5 %fusion.refs_0_ = f32[8,256,256]{2,1,0:T(8,128)} fusion(bf16[8,256,2049]{2,1,0:T(8,128)(2,1)} %group_rows.7, bf16[8,256,2049]{1,0,2:T(8,128)(2,1)S(1)} %slice-done.3), kind=kOutput, calls=%fused_computation | convolution fusion | flops 2148532224 | bytes 18882560 | tf_op jit(solution)/shard_map/sgk,shk->sgh/dot_general | solution.py:104
  100.1 4.2 %band_rows.5 = f32[16,32,8,128]{3,2,1,0:T(8,128)} custom-call(f32[1,128]{1,0:T(1,128)} %pad_bitcast_fusion.own_ref, f32[8,256,256]{2,1,0:T(8,128)} %fusion.refs_0_), custom_call_target="tpu_custom_call" | custom-call | bytes 4194304 | tf_op jit(solution)/shard_map/band_rows/pallas_call | solution.py:85
  104.3 71.0 %all-to-all-done.2.refs_1_ = f32[16,32,16,128]{3,2,1,0:T(8,128)} async-done(((f32[16,32,16,128]{3,2,1,0:T(8,128)}), f32[16,32,16,128]{3,2,1,0:T(8,128)}, u32[]{:S(2)}, u32[]{:S(2)}) %all-to-all-start.2) | async-done | bytes 4194336 | tf_op jit(solution)/shard_map/all_to_all | solution.py:195
  175.2 4.8 %all-to-all-start.1 = ((f32[16,32,8,128]{3,2,1,0:T(8,128)}), f32[16,32,8,128]{3,2,1,0:T(8,128)}, u32[]{:S(2)}, u32[]{:S(2)}) async-start(f32[16,32,8,128]{3,2,1,0:T(8,128)} %band_rows.5), calls=%async_computation.1 | async-start | bytes 4194304 | tf_op jit(solution)/shard_map/all_to_all | solution.py:195
  180.0 0.0 copy-done
  180.0 0.1 slice.35
  180.1 0.1 fusion.8
  180.2 0.7 reshape.14.pairs_ref
  180.9 0.1 reshape.12
  180.9 0.1 reshape.11
  181.1 0.8 copy.34.pairs_ref
  181.9 11.5 %place_columns.2.refs_1_ = f32[32,64,1024]{2,1,0:T(8,128)} custom-call(s32[1]{0:T(128)} %bitcast.flip_ref, s32[384,1]{1,0:T(8,128)} %copy.34.pairs_ref, f32[16,33,8,128]{3,2,1,0:T(8,128)} %copy-done, f32[16,32,16,128]{3,2,1,0:T(8,128)} %all-to-all-done.2.refs_1_), custom_call_target="tpu_custom_call" | custom-call | flops 1610612736 | bytes 33554432 | tf_op jit(solution)/shard_map/place_columns/pallas_call | solution.py:157
  193.4 34.2 %all-to-all-done.1.refs_0_ = f32[16,32,8,128]{3,2,1,0:T(8,128)} async-done(((f32[16,32,8,128]{3,2,1,0:T(8,128)}), f32[16,32,8,128]{3,2,1,0:T(8,128)}, u32[]{:S(2)}, u32[]{:S(2)}) %all-to-all-start.1) | async-done | bytes 2097184 | tf_op jit(solution)/shard_map/all_to_all | solution.py:195
  227.5 11.1 %place_columns.3 = f32[32,64,1024]{2,1,0:T(8,128)} custom-call(s32[1]{0:T(128)} %bitcast.flip_ref, s32[128,1]{1,0:T(8,128)} %reshape.14.pairs_ref, f32[16,32,8,128]{3,2,1,0:T(8,128)} %all-to-all-done.1.refs_0_, f32[32,64,1024]{2,1,0:T(8,128)} %place_columns.2.refs_1_), custom_call_target="tpu_custom_call" | custom-call | flops 536870912 | bytes 33554432 | tf_op jit(solution)/shard_map/place_columns/pallas_call | solution.py:157
  (2 shorter events, 0.0 us)
Async XLA Ops:
  7.6 3.4 %slice-start = ((bf16[32,256,2049]{1,0,2:T(8,128)(2,1)}), bf16[8,256,2049]{1,0,2:T(8,128)(2,1)S(1)}, s32[]{:S(2)}) async-start(bf16[32,256,2049]{1,0,2:T(8,128)(2,1)} %param.4), calls=%async_computation.3 | async-start | bytes 16785408 | tf_op jit(solution)/shard_map/slice | solution.py:103
  22.6 55.3 %all-to-all-start = ((f32[16,33,8,128]{3,2,1,0:T(8,128)}), f32[16,33,8,128]{3,2,1,0:T(8,128)S(1)}, u32[]{:S(2)}, u32[]{:S(2)}) async-start(f32[16,33,8,128]{3,2,1,0:T(8,128)} %band_rows.3), calls=%async_computation | async-start | bytes 4325376 | tf_op jit(solution)/shard_map/all_to_all | solution.py:195
  35.6 3.4 %slice-start.1 = ((bf16[32,256,2049]{1,0,2:T(8,128)(2,1)}), bf16[8,256,2049]{1,0,2:T(8,128)(2,1)S(1)}, s32[]{:S(2)}) async-start(bf16[32,256,2049]{1,0,2:T(8,128)(2,1)} %param.4), calls=%async_computation.4 | async-start | bytes 16785408 | tf_op jit(solution)/shard_map/slice | solution.py:103
  53.0 3.4 %slice-start.2 = ((bf16[32,256,2049]{1,0,2:T(8,128)(2,1)}), bf16[8,256,2049]{1,0,2:T(8,128)(2,1)S(1)}, s32[]{:S(2)}) async-start(bf16[32,256,2049]{1,0,2:T(8,128)(2,1)} %param.4), calls=%async_computation.5 | async-start | bytes 16785408 | tf_op jit(solution)/shard_map/slice | solution.py:103
  78.0 102.0 %copy-start = (f32[16,33,8,128]{3,2,1,0:T(8,128)}, f32[16,33,8,128]{3,2,1,0:T(8,128)S(1)}, u32[]{:S(2)}) copy-start(f32[16,33,8,128]{3,2,1,0:T(8,128)S(1)} %all-to-all-done.refs_0_) | copy-start | bytes 6488068
  78.0 97.2 %all-to-all-start.2 = ((f32[16,32,16,128]{3,2,1,0:T(8,128)}), f32[16,32,16,128]{3,2,1,0:T(8,128)}, u32[]{:S(2)}, u32[]{:S(2)}) async-start(f32[16,32,16,128]{3,2,1,0:T(8,128)} %band_rows.4), calls=%async_computation.2 | async-start | bytes 8388608 | tf_op jit(solution)/shard_map/all_to_all | solution.py:195
  89.2 3.4 %slice-start.3 = ((bf16[32,256,2049]{1,0,2:T(8,128)(2,1)}), bf16[8,256,2049]{1,0,2:T(8,128)(2,1)S(1)}, s32[]{:S(2)}) async-start(bf16[32,256,2049]{1,0,2:T(8,128)(2,1)} %param.4), calls=%async_computation.6 | async-start | bytes 16785408 | tf_op jit(solution)/shard_map/slice | solution.py:103
  175.2 52.3 %all-to-all-start.1 = ((f32[16,32,8,128]{3,2,1,0:T(8,128)}), f32[16,32,8,128]{3,2,1,0:T(8,128)}, u32[]{:S(2)}, u32[]{:S(2)}) async-start(f32[16,32,8,128]{3,2,1,0:T(8,128)} %band_rows.5), calls=%async_computation.1 | async-start | bytes 4194304 | tf_op jit(solution)/shard_map/all_to_all | solution.py:195
where the time goes:
time: 240 us; the launch traced here: 239 us
  waiting for transfers between devices  113 us (47%)
  Pallas kernels  63.4 us (26%)
  matrix products  30 us (12%)
  starting transfers between devices  16.1 us (7%)
  local copies, waits for them, and re-layouts  15.9 us (7%)
    all_to_all x3, waiting for transfers between devices, shards(): received.append(lax.all_to_all(rows, 'ma', 0, 0, tiled=True))  113 us
    dot_general x4, matrix products, chunk_rows(): jnp.einsum('sgk,shk->sgh', groups, functions, preferred_element_type=jnp....  30 us
    pallas_call x4, Pallas kernels, group_rows(): pl.pallas_call(functools.partial(group_kernel, start=start), grid_spec=pl...  25.8 us
    pallas_call x2, Pallas kernels, place_columns(): pl.pallas_call(functools.partial(place_kernel, held=held), grid_spec=pltp...  22.5 us
    all_to_all x3, starting transfers between devices, shards(): received.append(lax.all_to_all(rows, 'ma', 0, 0, tiled=True))  16.1 us
    pallas_call x3, Pallas kernels, band_rows(): pl.pallas_call(functools.partial(band_kernel, band=band), grid=(2,), in_s...  15 us
    slice x8, local copies, waits for them, and re-layouts, chunk_rows(): functions = lax.optimization_barrier(legendre[start:start + part])  13.5 us
  transfers between devices with their start and end apart: 3, of which 3 were waited for; matrix products, arithmetic and copies ran while one was open for 10% of the time, Pallas kernels for 17%

commit v1 on v0

v1 whole, which is shorter than its diff:
```python
import functools

import jax
import jax.numpy as jnp
from jax import lax
from jax.experimental import pallas as pl
from jax.experimental.pallas import tpu as pltpu
from jax.sharding import PartitionSpec as P

MESH = pl.DeviceIdType.MESH
BUFFERS = 3
LOADS = 4
SPAN = 256
CHUNK_ROWS = 4
EARLY_PART = 2


def mask_groups(first_len, coeff_ref, out_ref):
    columns = coeff_ref.shape[0]
    width = out_ref.shape[1]
    pack = 16
    entry = lax.broadcasted_iota(jnp.int32, (pack, width), 1)
    first = entry < first_len
    odd_gap = (jnp.where(first, entry, entry - first_len) & 1) == 1
    sign = jnp.where(odd_gap, -1.0, 1.0)
    scales = [
        jnp.where(first, 1.0, 0.0),
        jnp.where(first, 0.0, 1.0),
        jnp.where(first, sign, 0.0),
        jnp.where(first, 0.0, sign),
    ]
    scales = [scale.astype(out_ref.dtype) for scale in scales]
    for low in range(0, columns, pack):
        values = coeff_ref[low:low + pack, :width]
        for index, scale in enumerate(scales):
            at = index * columns + low
            out_ref[at:at + pack, :] = values * scale


def last_entries(first_len, coeff_ref, row_of, start):
    columns, width = coeff_ref.shape
    total = 0.0
    for entry in range(start, width):
        first = entry < first_len
        gap = jnp.where(first, entry, entry - first_len)
        sign = jnp.where((gap & 1) == 1, -1.0, 1.0)
        outer = coeff_ref[:, entry:entry + 1].astype(jnp.float32) * row_of(entry - start)
        kinds = [jnp.where(first, 1.0, 0.0), jnp.where(first, 0.0, 1.0)]
        kinds += [kind * sign for kind in kinds]
        total += jnp.concatenate([outer * kind for kind in kinds], axis=0)
    return total


def synthesis_kernel(
    assign_ref, coeffs_ref, legendre_ref, out_ref,
    coeff_buf, legendre_buf, rest, rest_wide, wide, functions, groups, send, recv, pair_row, pair_rows, pair_columns, place, high_rows, low_rows,
    coeff_sem, span_sem, rest_sem, send_sem, recv_sem, *, devices, early, chunk,
):
    me = lax.axis_index("ma")
    half = devices // 2
    side = me // half
    slots, columns, width = coeffs_ref.shape
    lat_half = legendre_ref.shape[2]
    held = functions.shape[0]
    spans = width // SPAN
    turns = 1 + slots // held
    lanes = 2 * columns
    band = send.shape[1] // slots
    total = devices * slots
    chunks = band // chunk
    by_slot = (devices, slots, band, lanes)
    outgoing = send.reshape(by_slot)
    incoming = recv.reshape(by_slot)

    def coeff_load(slot):
        buf = lax.rem(slot, BUFFERS)
        return pltpu.make_async_copy(coeffs_ref.at[slot], coeff_buf.at[buf], coeff_sem.at[buf])

    def span_load(index):
        buf = lax.rem(index, LOADS)
        group = jnp.maximum(index // spans - 1, 0)
        rows = pl.ds(lax.rem(index, spans) * SPAN, SPAN)
        source = legendre_ref.at[rows, pl.ds(pl.multiple_of(group * held, held), held), :]
        return pltpu.make_async_copy(source, legendre_buf.at[buf], span_sem.at[buf])

    def unpack(turn, members):
        def span_step(span, carry):
            index = turn * spans + span
            span_load(index).wait()
            buf = lax.rem(index, LOADS)
            for low in range(0, lat_half, 128):
                block = legendre_buf[buf, :, :, low:low + 128].astype(jnp.float32)
                wide[low // 128] = block.reshape(SPAN * held, 128)

            @pl.when(index + LOADS < turns * spans)
            def _():
                span_load(index + LOADS).start()

            at = pl.ds(pl.multiple_of(span * SPAN, SPAN), SPAN)
            for member in members:
                for low in range(0, lat_half, 128):
                    rows = wide[low // 128, pl.ds(member, SPAN, stride=held), :]
                    functions[member, at, low:low + 128] = rows.astype(functions.dtype)
            return carry

        lax.fori_loop(0, spans, span_step, 0)

    def for_peers(act):
        def across(k, carry):
            act((1 - side) * half + lax.rem(me + k, half))
            return carry

        def within(k, carry):
            act(side * half + lax.rem(me + k, half))
            return carry

        lax.fori_loop(0, half, across, 0)
        lax.fori_loop(1, half, within, 0)

    def copy(source, target, group, peer):
        return pltpu.make_async_remote_copy(
            src_ref=source,
            dst_ref=target,
            send_sem=send_sem.at[group],
            recv_sem=recv_sem.at[group],
            device_id={"ma": peer},
            device_id_type=MESH,
        )

    def compute(slot, member):
        coeff_load(slot).wait()
        buf = lax.rem(slot, BUFFERS)
        pair = assign_ref[slot]
        lane = lax.broadcasted_iota(jnp.int32, pair_row.shape, 1)
        pair_row[...] = jnp.where(lane == slot, pair, pair_row[...])
        first_len = width - 1 - pair
        mask_groups(first_len, coeff_buf.at[buf], groups)
        value = jnp.dot(groups[...], functions[member], preferred_element_type=jnp.float32)
        value += last_entries(first_len, coeff_buf.at[buf], lambda n: rest_wide[n, pl.ds(slot, 1), :], spans * SPAN)
        value = value.T
        at = pl.ds(pl.multiple_of(slot * band, band), band)
        for block in range(half):
            rows = slice(block * band, (block + 1) * band)
            send[block, at, :] = value[rows, :lanes]
            send[devices - 1 - block, at, :] = value[rows, lanes:]
        recv[me, at, :] = send[me, at, :]

        @pl.when(slot + BUFFERS < slots)
        def _():
            coeff_load(slot + BUFFERS).start()

    def send_slot(slot):
        for_peers(lambda peer: copy(outgoing.at[peer, slot], incoming.at[me, slot], 0, peer).start())

    def late(ref, device, first_row):
        return ref.at[device, pl.ds(early, slots - early), pl.ds(first_row, chunk), :]

    def send_chunk(index):
        row = index * chunk
        for_peers(lambda peer: copy(late(outgoing, peer, row), late(incoming, me, row), 1 + index, peer).start())

    for index in range(min(LOADS, turns * spans)):
        span_load(index).start()
    rest_load = pltpu.make_async_copy(legendre_ref.at[pl.ds(spans * SPAN, width - spans * SPAN)], rest, rest_sem)
    rest_load.start()
    for slot in range(min(BUFFERS, slots)):
        coeff_load(slot).start()
    barrier = pltpu.get_barrier_semaphore()
    for_peers(lambda peer: pl.semaphore_signal(barrier, inc=1, device_id={"ma": peer}, device_id_type=MESH))
    pair_row[...] = jnp.zeros_like(pair_row)
    rest_load.wait()
    rest_wide[...] = rest[...].astype(jnp.float32)
    unpack(0, [0])
    compute(0, 0)
    pl.semaphore_wait(barrier, devices - 1)
    send_slot(0)
    unpack(1, range(1, held))

    def member_step(group):
        def step(member, carry):
            slot = group * held + member
            compute(slot, member)

            @pl.when(slot < early)
            def _():
                send_slot(slot)

            return carry

        return step

    lax.fori_loop(1, held, member_step(0), 0)

    def group_step(group, carry):
        unpack(group + 1, range(held))
        lax.fori_loop(0, held, member_step(group), 0)
        return carry

    lax.fori_loop(1, slots // held, group_step, 0)

    pairs_group = 1 + chunks
    for_peers(lambda peer: copy(pair_row, pair_rows.at[me], pairs_group, peer).start())
    pair_rows[me] = pair_row[...]

    def chunk_step(index, carry):
        send_chunk(index)
        return carry

    lax.fori_loop(0, chunks, chunk_step, 0)

    others = pl.ds(0, devices - 1)
    whole = lambda ref: ref.at[others, pl.ds(0, early)]
    part = lambda ref, index: ref.at[others, pl.ds(early, slots - early), pl.ds(index * chunk, chunk), :]

    def wait_bytes(ref, sem):
        pltpu.make_async_copy(ref, ref, sem).wait()

    wait_bytes(pair_rows.at[others], recv_sem.at[pairs_group])

    def column_step(device, carry):
        row = pair_rows[device].astype(jnp.float32)
        rows = jnp.broadcast_to(row, (slots, row.shape[-1]))
        own = lax.broadcasted_iota(jnp.int32, rows.shape, 0) == lax.broadcasted_iota(jnp.int32, rows.shape, 1)
        column = jnp.sum(jnp.where(own, rows, 0.0), axis=1, keepdims=True)
        at = pl.ds(pl.multiple_of(device * slots, slots), slots)
        pair_columns[at, :] = jnp.broadcast_to(column, (slots, pair_columns.shape[1]))
        return carry

    lax.fori_loop(0, devices, column_step, 0)
    step = 64
    lane = lax.broadcasted_iota(jnp.int32, (step, total), 1)
    for low in range(0, total, step):
        pairs = pair_columns[low:low + step, :1].astype(jnp.int32)
        place[0, low:low + step, :] = (pairs == lane).astype(jnp.float32).astype(jnp.bfloat16)
        place[1, low:low + step, :] = (total - 1 - pairs == lane).astype(jnp.float32).astype(jnp.bfloat16)

    wait_bytes(whole(incoming), recv_sem.at[0])
    flat = recv.reshape(devices * slots * band, lanes)

    def place_step(index, carry):
        wait_bytes(part(incoming, index), recv_sem.at[1 + index])
        for i in range(chunk):
            row = index * chunk + i
            values = flat[pl.ds(row, total, stride=band), :].T
            high = values.astype(jnp.bfloat16)
            low = (values - high.astype(jnp.float32)).astype(jnp.bfloat16)
            for w in range(2):
                at = slice(i * columns, (i + 1) * columns)
                high_rows[w, at, :] = high[w * columns:(w + 1) * columns]
                low_rows[w, at, :] = low[w * columns:(w + 1) * columns]
        for w in range(2):
            placed = jnp.dot(high_rows[w], place[w], preferred_element_type=jnp.float32)
            placed += jnp.dot(low_rows[w], place[w], preferred_element_type=jnp.float32)
            for i in range(chunk):
                row = index * chunk + i
                to = row + side * (band - 1 - 2 * row)
                out_ref[to, :, w * total:(w + 1) * total] = placed[i * columns:(i + 1) * columns]
        return carry

    lax.fori_loop(0, chunks, place_step, 0)

    wait_bytes(whole(outgoing), send_sem.at[0])

    def drain_step(index, carry):
        wait_bytes(part(outgoing, index), send_sem.at[1 + index])
        return carry

    lax.fori_loop(0, chunks, drain_step, 0)
    wait_bytes(pair_rows.at[others], send_sem.at[pairs_group])


def shards(coeffs, legendre, assign):
    devices = lax.axis_size("ma")
    slots, columns, width = coeffs.shape
    lat_half = legendre.shape[1]
    band = 2 * lat_half // devices
    total = devices * slots
    lanes = 2 * columns
    chunk = min(CHUNK_ROWS, band)
    early = max(slots // EARLY_PART, 1)
    groups = 2 + band // chunk
    held = min(8, slots)
    main = width // SPAN * SPAN
    return pl.pallas_call(
        functools.partial(synthesis_kernel, devices=devices, early=early, chunk=chunk),
        out_shape=jax.ShapeDtypeStruct((band, columns, 2 * total), jnp.float32),
        in_specs=[
            pl.BlockSpec(memory_space=pltpu.SMEM),
            pl.BlockSpec(memory_space=pl.ANY),
            pl.BlockSpec(memory_space=pl.ANY),
        ],
        out_specs=pl.BlockSpec(memory_space=pltpu.VMEM),
        scratch_shapes=[
            pltpu.VMEM((BUFFERS, columns, width), jnp.bfloat16),
            pltpu.VMEM((LOADS, SPAN, held, lat_half), jnp.bfloat16),
            pltpu.VMEM((width - main, slots, lat_half), jnp.bfloat16),
            pltpu.VMEM((width - main, slots, lat_half), jnp.float32),
            pltpu.VMEM((lat_half // 128, SPAN * held, 128), jnp.float32),
            pltpu.VMEM((held, main, lat_half), jnp.bfloat16),
            pltpu.VMEM((4 * columns, main), jnp.bfloat16),
            pltpu.VMEM((devices, slots * band, lanes), jnp.float32),
            pltpu.VMEM((devices, slots * band, lanes), jnp.float32),
            pltpu.VMEM((1, lanes), jnp.int32),
            pltpu.VMEM((devices, 1, lanes), jnp.int32),
            pltpu.VMEM((total, lanes), jnp.float32),
            pltpu.VMEM((2, total, total), jnp.bfloat16),
            pltpu.VMEM((2, chunk * columns, total), jnp.bfloat16),
            pltpu.VMEM((2, chunk * columns, total), jnp.bfloat16),
            pltpu.SemaphoreType.DMA((BUFFERS,)),
            pltpu.SemaphoreType.DMA((LOADS,)),
            pltpu.SemaphoreType.DMA,
            pltpu.SemaphoreType.DMA((groups,)),
            pltpu.SemaphoreType.DMA((groups,)),
        ],
        compiler_params=pltpu.CompilerParams(
            collective_id=0, has_side_effects=True, vmem_limit_bytes=56 * 1024 * 1024
        ),
        name="synthesis",
    )(assign, coeffs, legendre.transpose(2, 0, 1))


def solution(mesh):
    return jax.shard_map(
        shards,
        mesh=mesh,
        in_specs=(P("ma", "af", None), P("ma", None, None), P("ma")),
        out_specs=P("ma", "af", None),
        check_vma=False,
    )
```

time: 240 us -> 205 us (0.85)
  Pallas kernels: 63.4 us -> 194 us
  waiting for transfers between devices: 113 us -> 0 us
  matrix products: 30 us -> 0 us
  starting transfers between devices: 16.1 us -> 0 us
  local copies, waits for them, and re-layouts: 15.9 us -> 8.44 us
    pallas_call x9 -> x1, Pallas kernels: 63.4 us -> 194 us  [shards(): pl.pallas_call(functools.partial(synthesis_kernel, devices=devices, early...]
    all_to_all x3 -> x0, waiting for transfers between devices: 113 us -> none  [shards(): received.append(lax.all_to_all(rows, 'ma', 0, 0, tiled=True))]
    dot_general x4 -> x0, matrix products: 30 us -> none  [chunk_rows(): jnp.einsum('sgk,shk->sgh', groups, functions, preferred_element_type=jnp....]
    all_to_all x3 -> x0, starting transfers between devices: 16.1 us -> none  [shards(): received.append(lax.all_to_all(rows, 'ma', 0, 0, tiled=True))]
    slice x10 -> x0, local copies, waits for them, and re-layouts: 13.7 us -> none  [the longest x8 13.5 us: chunk_rows(): functions = lax.optimization_barrier(legendre[start:start + part])]
    unnamed x2 -> x1, local copies, waits for them, and re-layouts: 0.01 us -> 8.44 us
  transfers between devices with their start and end apart: 3 -> 0, of which waited for: 3 -> 0; matrix products, arithmetic and copies ran while one was open for 10% -> 0% of each run, Pallas kernels for 17% -> 0%
where the time goes in v1:
time: 205 us; the launch traced here: 202 us
  Pallas kernels  194 us (95%)
  local copies, waits for them, and re-layouts  8.44 us (4%)
    pallas_call x1, Pallas kernels, shards(): pl.pallas_call(functools.partial(synthesis_kernel, devices=devices, early...  194 us
    unnamed x1, local copies, waits for them, and re-layouts  8.44 us

profile of v1, /device:TPU:15, one launch (start us, length us, event | category | flops | bytes accessed | tf_op | source)
XLA Modules:
  0.0 202.0 jit_solution(1278109805457561926)
XLA Ops:
  0.0 193.5 %synthesis.1 = f32[32,64,1024]{2,1,0:T(8,128)} custom-call(s32[32]{0:T(128)} %assign_ref.1, bf16[32,64,2049]{2,1,0:T(8,128)(2,1)} %coeffs_ref.1, bf16[2049,32,256]{2,1,0:T(8,128)(2,1)} %bitcast.1), custom_call_target="tpu_custom_call" | custom-call | tf_op jit(solution)/shard_map/synthesis/pallas_call | solution.py:284
  193.5 8.4 %copy.5 = f32[32,64,1024]{2,1,0:T(8,128)} copy(f32[32,64,1024]{2,1,0:T(8,128)} %synthesis.1) | data formatting | bytes 16777216

commit v2 on v1

--- a/solution.py
+++ b/solution.py
@@ -9,9 +9,10 @@
 
 MESH = pl.DeviceIdType.MESH
 BUFFERS = 3
-LOADS = 4
+LOADS = 8
+NARROW = 2
 SPAN = 256
-CHUNK_ROWS = 4
+CHUNK_ROWS = 2
 EARLY_PART = 2
 
 
@@ -64,6 +65,8 @@
     held = functions.shape[0]
     spans = width // SPAN
     turns = 1 + slots // held
+    parts = held // NARROW
+    share = SPAN // parts
     lanes = 2 * columns
     band = send.shape[1] // slots
     total = devices * slots
@@ -78,19 +81,63 @@
 
     def span_load(index):
         buf = lax.rem(index, LOADS)
+        rows = pl.ds(lax.rem(index, spans) * SPAN, SPAN)
         group = jnp.maximum(index // spans - 1, 0)
-        rows = pl.ds(lax.rem(index, spans) * SPAN, SPAN)
         source = legendre_ref.at[rows, pl.ds(pl.multiple_of(group * held, held), held), :]
         return pltpu.make_async_copy(source, legendre_buf.at[buf], span_sem.at[buf])
+
+    def narrow_loads(span):
+        buf = lax.rem(span, LOADS)
+        return [
+            pltpu.make_async_copy(
+                legendre_ref.at[pl.ds(span * SPAN + part * share, share), pl.ds(0, NARROW), :],
+                legendre_buf.at[buf, pl.ds(0, share), pl.ds(part * NARROW, NARROW), :],
+                span_sem.at[buf],
+            )
+            for part in range(parts)
+        ]
+
+    def widen(buf, rows):
+        for low in range(0, lat_half, 128):
+            block = legendre_buf[buf, :rows, :, low:low + 128].astype(jnp.float32)
+            wide[low // 128, :rows * held] = block.reshape(rows * held, 128)
+
+    def pick(member, at, first, rows):
+        for low in range(0, lat_half, 128):
+            block = wide[low // 128, pl.ds(first, rows, stride=held), :]
+            functions[member, at, low:low + 128] = block.astype(functions.dtype)
+
+    def unpack_narrow():
+        def span_step(span, carry):
+            buf = lax.rem(span, LOADS)
+            landed = legendre_buf.at[buf, pl.ds(0, share)]
+            pltpu.make_async_copy(landed, landed, span_sem.at[buf]).wait()
+            widen(buf, share)
+            later = span + LOADS
+
+            @pl.when(later < spans)
+            def _():
+                for load in narrow_loads(later):
+                    load.start()
+
+            @pl.when(later >= spans)
+            def _():
+                span_load(later).start()
+
+            for member in range(NARROW):
+                for part in range(parts):
+                    at = pl.ds(pl.multiple_of(span * SPAN + part * share, share), share)
+                    pick(member, at, part * NARROW + member, share)
+            return carry
+
+        lax.fori_loop(0, spans, span_step, 0)
 
     def unpack(turn, members):
         def span_step(span, carry):
             index = turn * spans + span
             span_load(index).wait()
             buf = lax.rem(index, LOADS)
-            for low in range(0, lat_half, 128):
-                block = legendre_buf[buf, :, :, low:low + 128].astype(jnp.float32)
-                wide[low // 128] = block.reshape(SPAN * held, 128)
+            widen(buf, SPAN)
 
             @pl.when(index + LOADS < turns * spans)
             def _():
@@ -98,9 +145,7 @@
 
             at = pl.ds(pl.multiple_of(span * SPAN, SPAN), SPAN)
             for member in members:
-                for low in range(0, lat_half, 128):
-                    rows = wide[low // 128, pl.ds(member, SPAN, stride=held), :]
-                    functions[member, at, low:low + 128] = rows.astype(functions.dtype)
+                pick(member, at, member, SPAN)
             return carry
 
         lax.fori_loop(0, spans, span_step, 0)
@@ -127,7 +172,7 @@
             device_id_type=MESH,
         )
 
-    def compute(slot, member):
+    def prepare(slot):
         coeff_load(slot).wait()
         buf = lax.rem(slot, BUFFERS)
         pair = assign_ref[slot]
@@ -135,6 +180,10 @@
         pair_row[...] = jnp.where(lane == slot, pair, pair_row[...])
         first_len = width - 1 - pair
         mask_groups(first_len, coeff_buf.at[buf], groups)
+
+    def compute(slot, member):
+        buf = lax.rem(slot, BUFFERS)
+        first_len = width - 1 - assign_ref[slot]
         value = jnp.dot(groups[...], functions[member], preferred_element_type=jnp.float32)
         value += last_entries(first_len, coeff_buf.at[buf], lambda n: rest_wide[n, pl.ds(slot, 1), :], spans * SPAN)
         value = value.T
@@ -159,26 +208,36 @@
         row = index * chunk
         for_peers(lambda peer: copy(late(outgoing, peer, row), late(incoming, me, row), 1 + index, peer).start())
 
-    for index in range(min(LOADS, turns * spans)):
+    coeff_load(0).start()
+    for index in range(min(LOADS, spans)):
+        for load in narrow_loads(index):
+            load.start()
+    for index in range(spans, LOADS):
         span_load(index).start()
     rest_load = pltpu.make_async_copy(legendre_ref.at[pl.ds(spans * SPAN, width - spans * SPAN)], rest, rest_sem)
     rest_load.start()
-    for slot in range(min(BUFFERS, slots)):
+    for slot in range(1, min(BUFFERS, slots)):
         coeff_load(slot).start()
     barrier = pltpu.get_barrier_semaphore()
     for_peers(lambda peer: pl.semaphore_signal(barrier, inc=1, device_id={"ma": peer}, device_id_type=MESH))
     pair_row[...] = jnp.zeros_like(pair_row)
+    prepare(0)
     rest_load.wait()
     rest_wide[...] = rest[...].astype(jnp.float32)
-    unpack(0, [0])
+    unpack_narrow()
     compute(0, 0)
     pl.semaphore_wait(barrier, devices - 1)
     send_slot(0)
-    unpack(1, range(1, held))
+    for slot in range(1, NARROW):
+        prepare(slot)
+        compute(slot, slot)
+        send_slot(slot)
+    unpack(1, range(NARROW, held))
 
     def member_step(group):
         def step(member, carry):
             slot = group * held + member
+            prepare(slot)
             compute(slot, member)
 
             @pl.when(slot < early)
@@ -189,7 +248,7 @@
 
         return step
 
-    lax.fori_loop(1, held, member_step(0), 0)
+    lax.fori_loop(NARROW, held, member_step(0), 0)
 
     def group_step(group, carry):
         unpack(group + 1, range(held))
@@ -283,7 +342,7 @@
     main = width // SPAN * SPAN
     return pl.pallas_call(
         functools.partial(synthesis_kernel, devices=devices, early=early, chunk=chunk),
-        out_shape=jax.ShapeDtypeStruct((band, columns, 2 * total), jnp.float32),
+        out_shape=pltpu.VMEM((band, columns, 2 * total), jnp.float32),
         in_specs=[
             pl.BlockSpec(memory_space=pltpu.SMEM),
             pl.BlockSpec(memory_space=pl.ANY),
@@ -313,7 +372,7 @@
             pltpu.SemaphoreType.DMA((groups,)),
         ],
         compiler_params=pltpu.CompilerParams(
-            collective_id=0, has_side_effects=True, vmem_limit_bytes=56 * 1024 * 1024
+            collective_id=0, has_side_effects=True, vmem_limit_bytes=50 * 1024 * 1024
         ),
         name="synthesis",
     )(assign, coeffs, legendre.transpose(2, 0, 1))

time: 205 us -> 195 us (0.951)
  Pallas kernels: 194 us -> 188 us
  local copies, waits for them, and re-layouts: 8.44 us -> 3.4 us
    pallas_call x1, Pallas kernels: 194 us -> 188 us  [shards(): pl.pallas_call(functools.partial(synthesis_kernel, devices=devices, early...]
    unnamed x1, local copies, waits for them, and re-layouts: 8.44 us -> 3.4 us
where the time goes in v2:
time: 195 us; the launch traced here: 192 us
  Pallas kernels  188 us (96%)
  local copies, waits for them, and re-layouts  3.4 us (2%)
    pallas_call x1, Pallas kernels, shards(): pl.pallas_call(functools.partial(synthesis_kernel, devices=devices, early...  188 us

profile of v2, /device:TPU:15, one launch (start us, length us, event | category | flops | bytes accessed | tf_op | source)
XLA Modules:
  0.0 191.6 jit_solution(15108793513516477180)
XLA Ops:
  0.0 188.2 %synthesis.1 = f32[32,64,1024]{2,1,0:T(8,128)S(1)} custom-call(s32[32]{0:T(128)} %assign_ref.1, bf16[32,64,2049]{2,1,0:T(8,128)(2,1)} %coeffs_ref.1, bf16[2049,32,256]{2,1,0:T(8,128)(2,1)} %bitcast.1), custom_call_target="tpu_custom_call" | custom-call | tf_op jit(solution)/shard_map/synthesis/pallas_call | solution.py:343
  188.2 3.4 %copy.5 = f32[32,64,1024]{2,1,0:T(8,128)} copy(f32[32,64,1024]{2,1,0:T(8,128)S(1)} %synthesis.1) | data formatting | bytes 16777216

commit v3 on v2

--- a/solution.py
+++ b/solution.py
@@ -52,14 +52,37 @@
     return total
 
 
+def place_rows(flat, place, high_rows, low_rows, first, count, band, store):
+    columns = high_rows.shape[1] // count
+    total = place.shape[1]
+
+    def split_row(i, carry):
+        values = flat[pl.ds(first + i, total, stride=band), :].T
+        high = values.astype(jnp.bfloat16)
+        low = (values - high.astype(jnp.float32)).astype(jnp.bfloat16)
+        at = pl.ds(pl.multiple_of(i * columns, columns), columns)
+        for w in range(2):
+            high_rows[w, at, :] = high[w * columns:(w + 1) * columns]
+            low_rows[w, at, :] = low[w * columns:(w + 1) * columns]
+        return carry
+
+    lax.fori_loop(0, count, split_row, 0)
+    for w in range(2):
+        placed = jnp.dot(high_rows[w], place[w], preferred_element_type=jnp.float32)
+        placed += jnp.dot(low_rows[w], place[w], preferred_element_type=jnp.float32)
+        for i in range(count):
+            store(i, w, placed[i * columns:(i + 1) * columns])
+
+
 def synthesis_kernel(
-    assign_ref, coeffs_ref, legendre_ref, out_ref,
-    coeff_buf, legendre_buf, rest, rest_wide, wide, functions, groups, send, recv, pair_row, pair_rows, pair_columns, place, high_rows, low_rows,
+    assign_ref, coeffs_ref, legendre_ref, out_ref, recv, place,
+    coeff_buf, legendre_buf, rest, rest_wide, wide, functions, groups, send, pair_row, pair_rows, pair_columns,
+    high_rows, low_rows,
     coeff_sem, span_sem, rest_sem, send_sem, recv_sem, *, devices, early, chunk,
 ):
     me = lax.axis_index("ma")
     half = devices // 2
-    side = me // half
+    side = lax.div(me, half)
     slots, columns, width = coeffs_ref.shape
     lat_half = legendre_ref.shape[2]
     held = functions.shape[0]
@@ -150,13 +173,22 @@
 
         lax.fori_loop(0, spans, span_step, 0)
 
+    def meet(k):
+        place_in_half = lax.rem(me, half)
+        if half & (half - 1):
+            return lax.rem(place_in_half + k, half)
+        partner = 0
+        for bit in [2 ** n for n in range(half.bit_length() - 1)]:
+            partner += lax.rem(lax.div(place_in_half, bit) + lax.div(k, bit), 2) * bit
+        return partner
+
     def for_peers(act):
         def across(k, carry):
-            act((1 - side) * half + lax.rem(me + k, half))
+            act((1 - side) * half + meet(k))
             return carry
 
         def within(k, carry):
-            act(side * half + lax.rem(me + k, half))
+            act(side * half + meet(k))
             return carry
 
         lax.fori_loop(0, half, across, 0)
@@ -209,22 +241,22 @@
         for_peers(lambda peer: copy(late(outgoing, peer, row), late(incoming, me, row), 1 + index, peer).start())
 
     coeff_load(0).start()
+    rest_load = pltpu.make_async_copy(legendre_ref.at[pl.ds(spans * SPAN, width - spans * SPAN)], rest, rest_sem)
+    rest_load.start()
     for index in range(min(LOADS, spans)):
         for load in narrow_loads(index):
             load.start()
     for index in range(spans, LOADS):
         span_load(index).start()
-    rest_load = pltpu.make_async_copy(legendre_ref.at[pl.ds(spans * SPAN, width - spans * SPAN)], rest, rest_sem)
-    rest_load.start()
     for slot in range(1, min(BUFFERS, slots)):
         coeff_load(slot).start()
     barrier = pltpu.get_barrier_semaphore()
     for_peers(lambda peer: pl.semaphore_signal(barrier, inc=1, device_id={"ma": peer}, device_id_type=MESH))
     pair_row[...] = jnp.zeros_like(pair_row)
     prepare(0)
+    unpack_narrow()
     rest_load.wait()
     rest_wide[...] = rest[...].astype(jnp.float32)
-    unpack_narrow()
     compute(0, 0)
     pl.semaphore_wait(barrier, devices - 1)
     send_slot(0)
@@ -298,25 +330,16 @@
 
     def place_step(index, carry):
         wait_bytes(part(incoming, index), recv_sem.at[1 + index])
-        for i in range(chunk):
+
+        def store(i, w, values):
             row = index * chunk + i
-            values = flat[pl.ds(row, total, stride=band), :].T
-            high = values.astype(jnp.bfloat16)
-            low = (values - high.astype(jnp.float32)).astype(jnp.bfloat16)
-            for w in range(2):
-                at = slice(i * columns, (i + 1) * columns)
-                high_rows[w, at, :] = high[w * columns:(w + 1) * columns]
-                low_rows[w, at, :] = low[w * columns:(w + 1) * columns]
-        for w in range(2):
-            placed = jnp.dot(high_rows[w], place[w], preferred_element_type=jnp.float32)
-            placed += jnp.dot(low_rows[w], place[w], preferred_element_type=jnp.float32)
-            for i in range(chunk):
-                row = index * chunk + i
-                to = row + side * (band - 1 - 2 * row)
-                out_ref[to, :, w * total:(w + 1) * total] = placed[i * columns:(i + 1) * columns]
-        return carry
-
-    lax.fori_loop(0, chunks, place_step, 0)
+            out_ref[row + side * (band - 1 - 2 * row), :, w * total:(w + 1) * total] = values
+
+        place_rows(flat, place, high_rows, low_rows, index * chunk, chunk, band, store)
+        return carry
+
+    lax.fori_loop(0, chunks - 1, place_step, 0)
+    wait_bytes(part(incoming, chunks - 1), recv_sem.at[chunks])
 
     wait_bytes(whole(outgoing), send_sem.at[0])
 
@@ -326,6 +349,27 @@
 
     lax.fori_loop(0, chunks, drain_step, 0)
     wait_bytes(pair_rows.at[others], send_sem.at[pairs_group])
+
+
+def deliver_kernel(placed_ref, recv, place, out_ref, last, high_rows, low_rows, sems, *, devices):
+    side = lax.div(lax.axis_index("ma"), devices // 2)
+    band = out_ref.shape[0]
+    count, _, total = last.shape
+    total //= 2
+    ready = pl.ds(side * count, band - count)
+    bulk = pltpu.make_async_copy(placed_ref.at[ready], out_ref.at[ready], sems.at[0])
+    bulk.start()
+    flat = recv.reshape(total * band, recv.shape[-1])
+
+    def store(i, w, values):
+        to = i + side * (count - 1 - 2 * i)
+        last[to, :, w * total:(w + 1) * total] = values
+
+    place_rows(flat, place, high_rows, low_rows, band - count, count, band, store)
+    tail = pltpu.make_async_copy(last, out_ref.at[pl.ds((1 - side) * (band - count), count)], sems.at[1])
+    tail.start()
+    bulk.wait()
+    tail.wait()
 
 
 def shards(coeffs, legendre, assign):
@@ -340,15 +384,19 @@
     groups = 2 + band // chunk
     held = min(8, slots)
     main = width // SPAN * SPAN
-    return pl.pallas_call(
+    placed, received, place = pl.pallas_call(
         functools.partial(synthesis_kernel, devices=devices, early=early, chunk=chunk),
-        out_shape=pltpu.VMEM((band, columns, 2 * total), jnp.float32),
+        out_shape=[
+            pltpu.VMEM((band, columns, 2 * total), jnp.float32),
+            pltpu.VMEM((devices, slots * band, lanes), jnp.float32),
+            pltpu.VMEM((2, total, total), jnp.bfloat16),
+        ],
         in_specs=[
             pl.BlockSpec(memory_space=pltpu.SMEM),
             pl.BlockSpec(memory_space=pl.ANY),
             pl.BlockSpec(memory_space=pl.ANY),
         ],
-        out_specs=pl.BlockSpec(memory_space=pltpu.VMEM),
+        out_specs=[pl.BlockSpec(memory_space=pltpu.VMEM)] * 3,
         scratch_shapes=[
             pltpu.VMEM((BUFFERS, columns, width), jnp.bfloat16),
             pltpu.VMEM((LOADS, SPAN, held, lat_half), jnp.bfloat16),
@@ -358,11 +406,9 @@
             pltpu.VMEM((held, main, lat_half), jnp.bfloat16),
             pltpu.VMEM((4 * columns, main), jnp.bfloat16),
             pltpu.VMEM((devices, slots * band, lanes), jnp.float32),
-            pltpu.VMEM((devices, slots * band, lanes), jnp.float32),
             pltpu.VMEM((1, lanes), jnp.int32),
             pltpu.VMEM((devices, 1, lanes), jnp.int32),
             pltpu.VMEM((total, lanes), jnp.float32),
-            pltpu.VMEM((2, total, total), jnp.bfloat16),
             pltpu.VMEM((2, chunk * columns, total), jnp.bfloat16),
             pltpu.VMEM((2, chunk * columns, total), jnp.bfloat16),
             pltpu.SemaphoreType.DMA((BUFFERS,)),
@@ -372,10 +418,24 @@
             pltpu.SemaphoreType.DMA((groups,)),
         ],
         compiler_params=pltpu.CompilerParams(
-            collective_id=0, has_side_effects=True, vmem_limit_bytes=50 * 1024 * 1024
+            collective_id=0, has_side_effects=True, vmem_limit_bytes=40 * 1024 * 1024
         ),
         name="synthesis",
     )(assign, coeffs, legendre.transpose(2, 0, 1))
+    return pl.pallas_call(
+        functools.partial(deliver_kernel, devices=devices),
+        out_shape=jax.ShapeDtypeStruct((band, columns, 2 * total), jnp.float32),
+        in_specs=[pl.BlockSpec(memory_space=pltpu.VMEM)] * 3,
+        out_specs=pl.BlockSpec(memory_space=pl.ANY),
+        scratch_shapes=[
+            pltpu.VMEM((chunk, columns, 2 * total), jnp.float32),
+            pltpu.VMEM((2, chunk * columns, total), jnp.bfloat16),
+            pltpu.VMEM((2, chunk * columns, total), jnp.bfloat16),
+            pltpu.SemaphoreType.DMA((2,)),
+        ],
+        compiler_params=pltpu.CompilerParams(vmem_limit_bytes=8 * 1024 * 1024),
+        name="deliver",
+    )(placed, received, place)
 
 
 def solution(mesh):

time: 195 us -> 193 us (0.990)
  local copies, waits for them, and re-layouts: 3.4 us -> 0 us
  Pallas kernels: 188 us -> 190 us
    pallas_call x0 -> x1, Pallas kernels: none -> 3.41 us  [shards(): pl.pallas_call(functools.partial(deliver_kernel, devices=devices), out_sh...]
    unnamed x1 -> x0, local copies, waits for them, and re-layouts: 3.4 us -> none
where the time goes in v3:
time: 193 us; the launch traced here: 190 us
  Pallas kernels  190 us (98%)
    pallas_call x1, Pallas kernels, shards(): pl.pallas_call(functools.partial(synthesis_kernel, devices=devices, early...  187 us

profile of v3, /device:TPU:15, one launch (start us, length us, event | category | flops | bytes accessed | tf_op | source)
XLA Modules:
  0.0 190.2 jit_solution(9599373150712297245)
XLA Ops:
  0.0 186.8 %synthesis.1 = (f32[32,64,1024]{2,1,0:T(8,128)S(1)}, f32[16,1024,128]{2,1,0:T(8,128)S(1)}, bf16[2,512,512]{2,1,0:T(8,128)(2,1)S(1)}) custom-call(s32[32]{0:T(128)} %assign_ref.1, bf16[32,64,2049]{2,1,0:T(8,128)(2,1)} %coeffs_ref.1, bf16[2049,32,256]{2,1,0:T(8,128)(2,1)} %bitcast.1), custom_call_target="tpu_custom_call" | custom-call | tf_op jit(solution)/shard_map/synthesis/pallas_call | solution.py:387
  186.8 3.4 %deliver.1 = f32[32,64,1024]{2,1,0:T(8,128)} custom-call(f32[32,64,1024]{2,1,0:T(8,128)S(1)} %get-tuple-element.8.placed_ref, f32[16,1024,128]{2,1,0:T(8,128)S(1)} %get-tuple-element.9.recv, bf16[2,512,512]{2,1,0:T(8,128)(2,1)S(1)} %get-tuple-element.10.place), custom_call_target="tpu_custom_call" | custom-call | tf_op jit(solution)/shard_map/deliver/pallas_call | solution.py:425

commit v4 on v3

--- a/solution.py
+++ b/solution.py
@@ -12,8 +12,8 @@
 LOADS = 8
 NARROW = 2
 SPAN = 256
-CHUNK_ROWS = 2
-EARLY_PART = 2
+CHUNK_ROWS = 4
+EARLY_PART = 4
 
 
 def mask_groups(first_len, coeff_ref, out_ref):
@@ -75,10 +75,10 @@
 
 
 def synthesis_kernel(
-    assign_ref, coeffs_ref, legendre_ref, out_ref, recv, place,
-    coeff_buf, legendre_buf, rest, rest_wide, wide, functions, groups, send, pair_row, pair_rows, pair_columns,
+    assign_hbm, coeffs_ref, legendre_ref, out_ref, recv, place,
+    assign_ref, coeff_buf, legendre_buf, rest, rest_wide, wide, functions, groups, send, pair_row, pair_rows, pair_columns,
     high_rows, low_rows,
-    coeff_sem, span_sem, rest_sem, send_sem, recv_sem, *, devices, early, chunk,
+    assign_sem, coeff_sem, span_sem, rest_sem, send_sem, recv_sem, *, devices, early, chunk,
 ):
     me = lax.axis_index("ma")
     half = devices // 2
@@ -240,6 +240,10 @@
         row = index * chunk
         for_peers(lambda peer: copy(late(outgoing, peer, row), late(incoming, me, row), 1 + index, peer).start())
 
+    barrier = pltpu.get_barrier_semaphore()
+    for_peers(lambda peer: pl.semaphore_signal(barrier, inc=1, device_id={"ma": peer}, device_id_type=MESH))
+    assign_load = pltpu.make_async_copy(assign_hbm, assign_ref, assign_sem)
+    assign_load.start()
     coeff_load(0).start()
     rest_load = pltpu.make_async_copy(legendre_ref.at[pl.ds(spans * SPAN, width - spans * SPAN)], rest, rest_sem)
     rest_load.start()
@@ -250,9 +254,8 @@
         span_load(index).start()
     for slot in range(1, min(BUFFERS, slots)):
         coeff_load(slot).start()
-    barrier = pltpu.get_barrier_semaphore()
-    for_peers(lambda peer: pl.semaphore_signal(barrier, inc=1, device_id={"ma": peer}, device_id_type=MESH))
     pair_row[...] = jnp.zeros_like(pair_row)
+    assign_load.wait()
     prepare(0)
     unpack_narrow()
     rest_load.wait()
@@ -380,7 +383,7 @@
     total = devices * slots
     lanes = 2 * columns
     chunk = min(CHUNK_ROWS, band)
-    early = max(slots // EARLY_PART, 1)
+    early = max(slots // EARLY_PART, NARROW)
     groups = 2 + band // chunk
     held = min(8, slots)
     main = width // SPAN * SPAN
@@ -392,12 +395,13 @@
             pltpu.VMEM((2, total, total), jnp.bfloat16),
         ],
         in_specs=[
-            pl.BlockSpec(memory_space=pltpu.SMEM),
+            pl.BlockSpec(memory_space=pl.ANY),
             pl.BlockSpec(memory_space=pl.ANY),
             pl.BlockSpec(memory_space=pl.ANY),
         ],
         out_specs=[pl.BlockSpec(memory_space=pltpu.VMEM)] * 3,
         scratch_shapes=[
+            pltpu.SMEM((slots,), jnp.int32),
             pltpu.VMEM((BUFFERS, columns, width), jnp.bfloat16),
             pltpu.VMEM((LOADS, SPAN, held, lat_half), jnp.bfloat16),
             pltpu.VMEM((width - main, slots, lat_half), jnp.bfloat16),
@@ -411,6 +415,7 @@
             pltpu.VMEM((total, lanes), jnp.float32),
             pltpu.VMEM((2, chunk * columns, total), jnp.bfloat16),
             pltpu.VMEM((2, chunk * columns, total), jnp.bfloat16),
+            pltpu.SemaphoreType.DMA,
             pltpu.SemaphoreType.DMA((BUFFERS,)),
             pltpu.SemaphoreType.DMA((LOADS,)),
             pltpu.SemaphoreType.DMA,

time: 193 us -> 191 us (0.990)
  no operation moved by 1% of the time
where the time goes in v4:
time: 191 us; the launch traced here: 189 us
  Pallas kernels  189 us (99%)
    pallas_call x1, Pallas kernels, shards(): pl.pallas_call(functools.partial(synthesis_kernel, devices=devices, early...  186 us

profile of v4, /device:TPU:15, one launch (start us, length us, event | category | flops | bytes accessed | tf_op | source)
XLA Modules:
  0.0 189.4 jit_solution(17861774791974241774)
XLA Ops:
  0.0 186.0 %synthesis.1 = (f32[32,64,1024]{2,1,0:T(8,128)S(1)}, f32[16,1024,128]{2,1,0:T(8,128)S(1)}, bf16[2,512,512]{2,1,0:T(8,128)(2,1)S(1)}) custom-call(s32[32]{0:T(128)} %assign_hbm.1, bf16[32,64,2049]{2,1,0:T(8,128)(2,1)} %coeffs_ref.1, bf16[2049,32,256]{2,1,0:T(8,128)(2,1)} %bitcast.1), custom_call_target="tpu_custom_call" | custom-call | tf_op jit(solution)/shard_map/synthesis/pallas_call | solution.py:390
  186.0 3.4 %deliver.1 = f32[32,64,1024]{2,1,0:T(8,128)} custom-call(f32[32,64,1024]{2,1,0:T(8,128)S(1)} %get-tuple-element.8.placed_ref, f32[16,1024,128]{2,1,0:T(8,128)S(1)} %get-tuple-element.9.recv, bf16[2,512,512]{2,1,0:T(8,128)(2,1)S(1)} %get-tuple-element.10.place), custom_call_target="tpu_custom_call" | custom-call | tf_op jit(solution)/shard_map/deliver/pallas_call | solution.py:430

commit v5 on v4

--- a/solution.py
+++ b/solution.py
@@ -275,9 +275,10 @@
             prepare(slot)
             compute(slot, member)
 
-            @pl.when(slot < early)
+            @pl.when(jnp.logical_and(slot < early, lax.rem(slot, 2) == 1))
             def _():
-                send_slot(slot)
+                pair = pl.ds(slot - 1, 2)
+                for_peers(lambda peer: copy(outgoing.at[peer, pair], incoming.at[me, pair], 0, peer).start())
 
             return carry
 
@@ -383,7 +384,7 @@
     total = devices * slots
     lanes = 2 * columns
     chunk = min(CHUNK_ROWS, band)
-    early = max(slots // EARLY_PART, NARROW)
+    early = max(slots // EARLY_PART // 2 * 2, NARROW)
     groups = 2 + band // chunk
     held = min(8, slots)
     main = width // SPAN * SPAN

time: 191 us -> 190 us (level)
  no operation moved by 1% of the time
where the time goes in v5:
time: 190 us; the launch traced here: 189 us
  Pallas kernels  189 us (99%)
    pallas_call x1, Pallas kernels, shards(): pl.pallas_call(functools.partial(synthesis_kernel, devices=devices, early...  186 us

profile of v5, /device:TPU:15, one launch (start us, length us, event | category | flops | bytes accessed | tf_op | source)
XLA Modules:
  0.0 189.3 jit_solution(9714199295699129399)
XLA Ops:
  0.0 185.9 %synthesis.1 = (f32[32,64,1024]{2,1,0:T(8,128)S(1)}, f32[16,1024,128]{2,1,0:T(8,128)S(1)}, bf16[2,512,512]{2,1,0:T(8,128)(2,1)S(1)}) custom-call(s32[32]{0:T(128)} %assign_hbm.1, bf16[32,64,2049]{2,1,0:T(8,128)(2,1)} %coeffs_ref.1, bf16[2049,32,256]{2,1,0:T(8,128)(2,1)} %bitcast.1), custom_call_target="tpu_custom_call" | custom-call | tf_op jit(solution)/shard_map/synthesis/pallas_call | solution.py:391
  185.9 3.4 %deliver.1 = f32[32,64,1024]{2,1,0:T(8,128)} custom-call(f32[32,64,1024]{2,1,0:T(8,128)S(1)} %get-tuple-element.8.placed_ref, f32[16,1024,128]{2,1,0:T(8,128)S(1)} %get-tuple-element.9.recv, bf16[2,512,512]{2,1,0:T(8,128)(2,1)S(1)} %get-tuple-element.10.place), custom_call_target="tpu_custom_call" | custom-call | tf_op jit(solution)/shard_map/deliver/pallas_call | solution.py:431
